TPU v7x, 32 devices: a whole 2x2x4 slice. The times are simulated.
32 devices in a mesh: row: 4 (over y, x), col: 8 (over z, core).
Axes of the slice: x: 2, y: 2, z: 4, core: 2. Of those that a mesh axis runs over, the one named last changes fastest.
Arguments:
- pair_rep: bfloat16 [256, 256, 128], P('row', 'col'), may hold values from -6 to 6
- proj_weight: bfloat16 [2, 4, 128, 128], replicated, may hold values from -0.5 to 0.5
- gate_weight: bfloat16 [2, 128, 128], replicated, may hold values from -0.5 to 0.5
- out_weight: bfloat16 [2, 128, 128], replicated, may hold values from -0.5 to 0.5
- in_gain: float32 [2, 128], replicated, may hold values from 0.1 to 1.9
- out_gain: float32 [2, 128], replicated, may hold values from 0.1 to 1.9
Outputs:
- updated_pair: bfloat16 [256, 256, 128], P('row', 'col')
All inputs are finite; a program needn't handle non-finite values.
Results may differ from a plain program's by a relative error of at most 0.011.
Values may be sent and summed in bfloat16 or wider, within the bound.
A program may use at most 64 MiB of HBM per device.

v0:
```python
import jax
import jax.numpy as jnp
from jax import lax
from jax.sharding import PartitionSpec as P

epsilon = 1e-05


def layer_norm(values, gain_row, reduce_axis):
    center = values - jnp.mean(values, axis=reduce_axis, keepdims=True)
    spread = jnp.mean(center * center, axis=reduce_axis, keepdims=True)
    return center * lax.rsqrt(spread + epsilon) * gain_row


def local(pair_rep, proj_weight, gate_weight, out_weight, in_gain, out_gain):
    current = pair_rep
    for update_index in range(2):
        widened = current.astype(jnp.float32)
        normed = layer_norm(widened, in_gain[update_index], 2).astype(jnp.bfloat16)
        projected = jnp.einsum(
            "ijc,pch->phij", normed, proj_weight[update_index], preferred_element_type=jnp.float32
        )
        left_hand = (jax.nn.sigmoid(projected[0]) * projected[1]).astype(jnp.bfloat16)
        right_hand = (jax.nn.sigmoid(projected[2]) * projected[3]).astype(jnp.bfloat16)
        gating = jax.nn.sigmoid(
            jnp.dot(normed, gate_weight[update_index], preferred_element_type=jnp.float32)
        )
        left_rows, right_rows = (
            lax.all_to_all(left_hand, "col", split_axis=0, concat_axis=2, tiled=True),
            lax.all_to_all(right_hand, "col", split_axis=0, concat_axis=2, tiled=True),
        )
        if update_index == 0:
            triangle = jnp.einsum(
                "gik,gjk->igj",
                left_rows,
                lax.all_gather(right_rows, "row", axis=1, tiled=True),
                preferred_element_type=jnp.float32,
            )
        else:
            left_columns = lax.all_to_all(left_rows, "row", split_axis=2, concat_axis=1, tiled=True)
            triangle = jnp.einsum(
                "gki,gkj->igj",
                left_columns,
                lax.all_gather(right_rows, "row", axis=1, tiled=True),
                preferred_element_type=jnp.float32,
            )
        returned = lax.all_to_all(
            triangle.astype(jnp.bfloat16), "col", split_axis=2, concat_axis=1, tiled=True
        )
        mixed_rows = layer_norm(
            returned.astype(jnp.float32), out_gain[update_index][None, :, None], 1
        ).astype(jnp.bfloat16)
        update = jnp.einsum(
            "ihj,hc->ijc", mixed_rows, out_weight[update_index], preferred_element_type=jnp.float32
        )
        current = (widened + gating * update).astype(jnp.bfloat16)
    return current


def solution(mesh):
    return jax.shard_map(
        local,
        mesh=mesh,
        in_specs=(P("row", "col", None), P(), P(), P(), P(), P()),
        out_specs=P("row", "col", None),
        check_vma=False,
    )
```

profile of v0, /device:TPU:0, one launch (start us, length us, event | category | flops | bytes accessed | tf_op | source)
XLA Modules:
  0.0 204.8 jit_solution(6984792394690389047)
XLA Ops:
  6.5 1.4 convert_reduce_fusion.1
  8.1 1.7 fusion.33
  9.9 0.8 slice_bitcast_fusion
  10.7 2.0 convolution_bitcast_fusion.1
  12.7 0.6 fusion.71
  13.3 1.7 copy.107
  15.0 0.7 reshape.116
  15.7 21.5 %all_to_all.108 = bf16[8,2,16384]{2,1,0:T(2,128)(2,1)S(1)} all-to-all(bf16[8,2,16384]{2,1,0:T(2,128)(2,1)S(1)} %reshape.116), channel_id=1, replica_groups=mesh['row'=4,'col'=8] {'col'}, dimensions={0} | all-to-all | bytes 1048576 | tf_op jit(solution)/shard_map/all_to_all | solution.py:30
  37.2 0.7 reshape.117
  37.9 1.1 copy.109
  39.1 1.7 copy.110
  40.8 0.7 reshape.118
  41.5 17.7 %all_to_all.109 = bf16[8,2,16384]{2,1,0:T(2,128)(2,1)S(1)} all-to-all(bf16[8,2,16384]{2,1,0:T(2,128)(2,1)S(1)} %reshape.118), channel_id=1, replica_groups=mesh['row'=4,'col'=8] {'col'}, dimensions={0} | all-to-all | bytes 1048576 | tf_op jit(solution)/shard_map/all_to_all | solution.py:29
  59.2 0.7 reshape.119
  60.0 13.3 %all-gather.3.cloned.1.call-done = bf16[16,256,256]{2,1,0:T(8,128)(2,1)} async-done(((bf16[16,64,256]{2,1,0:T(8,128)(2,1)}), bf16[16,256,256]{2,1,0:T(8,128)(2,1)}) %all-gather.3.cloned.1.call-update) | async-done | bytes 2097168 | tf_op jit(solution)/shard_map/all_gather | solution.py:36
  73.4 2.3 %fusion.29 = bf16[64,16,256]{2,0,1:T(8,128)(2,1)S(1)} fusion(bf16[16,256,256]{2,1,0:T(8,128)(2,1)} %all-gather.3.cloned.1.call-done, bf16[16,64,256]{1,2,0:T(8,128)(2,1)S(1)} %bitcast.149), kind=kOutput, calls=%fused_computation.43 | convolution fusion | flops 134479872 | bytes 3145728 | tf_op jit(solution)/shard_map/gik,gjk->igj/dot_general | solution.py:33
  75.7 1.0 copy.113
  76.7 1.5 reshape.120
  78.2 4.6 %all-to-all-start.2 = ((bf16[8,2,16384]{2,1,0:T(2,128)(2,1)}), bf16[8,2,16384]{2,1,0:T(2,128)(2,1)S(1)}, u32[]{:S(2)}, u32[]{:S(2)}) async-start(bf16[8,2,16384]{2,1,0:T(2,128)(2,1)} %reshape.120), calls=%async_computation.2 | async-start | bytes 1048576 | tf_op jit(solution)/shard_map/all_to_all | solution.py:47
  83.2 14.9 %all-to-all-done.2 = bf16[8,2,16384]{2,1,0:T(2,128)(2,1)S(1)} async-done(((bf16[8,2,16384]{2,1,0:T(2,128)(2,1)}), bf16[8,2,16384]{2,1,0:T(2,128)(2,1)S(1)}, u32[]{:S(2)}, u32[]{:S(2)}) %all-to-all-start.2) | async-done | bytes 524320 | tf_op jit(solution)/shard_map/all_to_all | solution.py:47
  98.1 0.7 reshape.121
  100.3 1.5 copy.117
  102.1 1.2 convert_reduce_fusion
  103.4 0.6 fusion.30
  104.3 0.8 convolution_bitcast_fusion
  105.6 1.7 copy.122
  107.3 0.7 reshape.126
  108.0 17.7 %all_to_all.110 = bf16[8,2,16384]{2,1,0:T(2,128)(2,1)S(1)} all-to-all(bf16[8,2,16384]{2,1,0:T(2,128)(2,1)S(1)} %reshape.126), channel_id=1, replica_groups=mesh['row'=4,'col'=8] {'col'}, dimensions={0} | all-to-all | bytes 1048576 | tf_op jit(solution)/shard_map/all_to_all | solution.py:30
  125.7 0.7 reshape.127
  126.5 1.1 copy.124
  127.7 1.7 copy.125
  129.4 0.7 reshape.122
  130.1 17.7 %all_to_all.111 = bf16[8,2,16384]{2,1,0:T(2,128)(2,1)S(1)} all-to-all(bf16[8,2,16384]{2,1,0:T(2,128)(2,1)S(1)} %reshape.122), channel_id=1, replica_groups=mesh['row'=4,'col'=8] {'col'}, dimensions={0} | all-to-all | bytes 1048576 | tf_op jit(solution)/shard_map/all_to_all | solution.py:29
  147.8 0.7 reshape.123
  148.6 0.7 copy.145
  149.3 0.9 reshape.124
  150.1 16.6 %all_to_all.112 = bf16[4,2,32768]{2,1,0:T(2,128)(2,1)S(1)} all-to-all(bf16[4,2,32768]{2,1,0:T(2,128)(2,1)S(1)} %reshape.124), channel_id=1, replica_groups=mesh['row'=4,'col'=8] {'row'}, dimensions={0} | all-to-all | bytes 1048576 | tf_op jit(solution)/shard_map/all_to_all | solution.py:40
  166.8 0.7 reshape.125
  167.5 0.8 copy.144
  168.3 0.7 all_to_all.99
  169.0 2.1 %fusion.28 = bf16[64,16,256]{2,0,1:T(8,128)(2,1)S(1)} fusion(bf16[16,256,64]{1,2,0:T(8,128)(2,1)S(1)} %all_to_all.99, bf16[16,256,256]{2,1,0:T(8,128)(2,1)} %all-gather.5.cloned.1.call-done), kind=kOutput, calls=%fused_computation.42 | convolution fusion | flops 134479872 | bytes 3145728 | tf_op jit(solution)/shard_map/gki,gkj->igj/dot_general | solution.py:41
  171.1 1.0 copy.130
  172.1 1.5 reshape.128
  173.6 3.5 %all-to-all-start.6 = ((bf16[8,2,16384]{2,1,0:T(2,128)(2,1)}), bf16[8,2,16384]{2,1,0:T(2,128)(2,1)S(1)}, u32[]{:S(2)}, u32[]{:S(2)}) async-start(bf16[8,2,16384]{2,1,0:T(2,128)(2,1)} %reshape.128), calls=%async_computation.6 | async-start | bytes 1048576 | tf_op jit(solution)/shard_map/all_to_all | solution.py:47
  177.2 15.1 %all-to-all-done.6 = bf16[8,2,16384]{2,1,0:T(2,128)(2,1)S(1)} async-done(((bf16[8,2,16384]{2,1,0:T(2,128)(2,1)}), bf16[8,2,16384]{2,1,0:T(2,128)(2,1)S(1)}, u32[]{:S(2)}, u32[]{:S(2)}) %all-to-all-start.6) | async-done | bytes 524320 | tf_op jit(solution)/shard_map/all_to_all | solution.py:47
  192.3 0.7 reshape.129
  194.4 1.5 copy.134
  196.2 1.7 fusion.23
  (53 shorter events, 5.6 us)
Async XLA Ops:
  6.5 66.8 %all-gather.3.cloned.1.call-start = ((), (), s32[]{:S(2)}) async-start(), calls=%async_computation.7 | async-start | bytes 2621440 | tf_op jit(solution)/shard_map/all_gather | solution.py:36
  75.7 7.3 %copy-start.3 = (f32[2,128]{1,0:T(2,128)S(1)}, f32[2,128]{1,0:T(2,128)}, u32[]{:S(2)}) copy-start(f32[2,128]{1,0:T(2,128)} %param.11) | copy-start | bytes 3076
  78.2 19.9 %all-to-all-start.2 = ((bf16[8,2,16384]{2,1,0:T(2,128)(2,1)}), bf16[8,2,16384]{2,1,0:T(2,128)(2,1)S(1)}, u32[]{:S(2)}, u32[]{:S(2)}) async-start(bf16[8,2,16384]{2,1,0:T(2,128)(2,1)} %reshape.120), calls=%async_computation.2 | async-start | bytes 1048576 | tf_op jit(solution)/shard_map/all_to_all | solution.py:47
  82.8 86.2 %all-gather.5.cloned.1.call-start = ((), (), s32[]{:S(2)}) async-start(), calls=%async_computation.8 | async-start | bytes 2621440 | tf_op jit(solution)/shard_map/all_gather | solution.py:44
  100.1 1.7 copy-start.2
  100.2 1.9 copy-start
  100.2 1.9 copy-start.4
  102.1 2.1 %copy-start.1 = (bf16[2,4,128,128]{3,2,1,0:T(8,128)(2,1)S(1)}, bf16[2,4,128,128]{3,2,1,0:T(8,128)(2,1)}, u32[]{:S(2)}) copy-start(bf16[2,4,128,128]{3,2,1,0:T(8,128)(2,1)} %param.7) | copy-start | bytes 786436
  173.6 18.8 %all-to-all-start.6 = ((bf16[8,2,16384]{2,1,0:T(2,128)(2,1)}), bf16[8,2,16384]{2,1,0:T(2,128)(2,1)S(1)}, u32[]{:S(2)}, u32[]{:S(2)}) async-start(bf16[8,2,16384]{2,1,0:T(2,128)(2,1)} %reshape.128), calls=%async_computation.6 | async-start | bytes 1048576 | tf_op jit(solution)/shard_map/all_to_all | solution.py:47
Sparse Core Ops, SparseCore 0:
  39.2 34.1 all-gather.2
  127.8 38.4 all-gather.4
where the time goes:
time: 205 us
  blocking collectives  91.3 us (45%)
  waiting for transfers between devices  43.4 us (21%)
  local copies, waits for them, and re-layouts  30.4 us (15%)
  between operations  13.8 us (7%)
  matrix products  10.6 us (5%)
  starting transfers between devices  8.32 us (4%)
  other arithmetic  6.98 us (3%)
    all_to_all x2, blocking collectives, local(): lax.all_to_all(right_hand, 'col', split_axis=0, concat_axis=2, tiled=True)  39.2 us
    all_to_all x2, blocking collectives, local(): lax.all_to_all(left_hand, 'col', split_axis=0, concat_axis=2, tiled=True)  35.5 us
    all_to_all x2, waiting for transfers between devices, local(): lax.all_to_all(triangle.astype(jnp.bfloat16), 'col', split_axis=2, concat...  30 us
    all_to_all x1, blocking collectives, local(): lax.all_to_all(left_rows, 'row', split_axis=2, concat_axis=1, tiled=True)  16.6 us
    all_gather x2, waiting for transfers between devices, local(): lax.all_gather(right_rows, 'row', axis=1, tiled=True)  13.4 us
    unnamed x24, local copies, waits for them, and re-layouts  11.3 us
    all_to_all x2, starting transfers between devices, local(): lax.all_to_all(triangle.astype(jnp.bfloat16), 'col', split_axis=2, concat...  8.1 us
  transfers between devices with their start and end apart: 4, of which 3 were waited for; matrix products, arithmetic and copies ran while one was open for 5% of the time, Pallas kernels for 0%

commit v1 on v0

v1 whole, which is shorter than its diff:
```python
import functools

import jax
import jax.numpy as jnp
from jax import lax
from jax.experimental import pallas as pl
from jax.experimental.pallas import tpu as pltpu
from jax.sharding import PartitionSpec as P

epsilon = 1e-05
LANES = 128
PACK = 16
f32 = jnp.float32
bf16 = jnp.bfloat16


def layer_norm(values, gain_row, reduce_axis):
    center = values - jnp.mean(values, axis=reduce_axis, keepdims=True)
    spread = jnp.mean(center * center, axis=reduce_axis, keepdims=True)
    return center * lax.rsqrt(spread + epsilon) * gain_row


def plain(pair_rep, proj_weight, gate_weight, out_weight, in_gain, out_gain):
    current = pair_rep
    for update_index in range(2):
        widened = current.astype(f32)
        normed = layer_norm(widened, in_gain[update_index], 2).astype(bf16)
        projected = jnp.einsum(
            "ijc,pch->phij", normed, proj_weight[update_index], preferred_element_type=f32
        )
        left_hand = (jax.nn.sigmoid(projected[0]) * projected[1]).astype(bf16)
        right_hand = (jax.nn.sigmoid(projected[2]) * projected[3]).astype(bf16)
        gating = jax.nn.sigmoid(
            jnp.dot(normed, gate_weight[update_index], preferred_element_type=f32)
        )
        left_rows, right_rows = (
            lax.all_to_all(left_hand, "col", split_axis=0, concat_axis=2, tiled=True),
            lax.all_to_all(right_hand, "col", split_axis=0, concat_axis=2, tiled=True),
        )
        if update_index == 0:
            triangle = jnp.einsum(
                "gik,gjk->igj",
                left_rows,
                lax.all_gather(right_rows, "row", axis=1, tiled=True),
                preferred_element_type=f32,
            )
        else:
            left_columns = lax.all_to_all(left_rows, "row", split_axis=2, concat_axis=1, tiled=True)
            triangle = jnp.einsum(
                "gki,gkj->igj",
                left_columns,
                lax.all_gather(right_rows, "row", axis=1, tiled=True),
                preferred_element_type=f32,
            )
        returned = lax.all_to_all(
            triangle.astype(bf16), "col", split_axis=2, concat_axis=1, tiled=True
        )
        mixed_rows = layer_norm(
            returned.astype(f32), out_gain[update_index][None, :, None], 1
        ).astype(bf16)
        update = jnp.einsum(
            "ihj,hc->ijc", mixed_rows, out_weight[update_index], preferred_element_type=f32
        )
        current = (widened + gating * update).astype(bf16)
    return current


def norm_columns(values, gain_column):
    scale = 1.0 / values.shape[0]
    center = values - jnp.sum(values, axis=0, keepdims=True) * scale
    spread = jnp.sum(center * center, axis=0, keepdims=True) * scale
    return center * lax.rsqrt(spread + epsilon) * gain_column


def kernel(rows, cols, x_ref, pw_ref, gw_ref, ow_ref, ig_ref, og_ref, o_ref,
           xt, nt, gt, tt, wt, gwt, owt, perm, shuffle, back,
           send_lr, recv_lr, send_t, recv_t, ml, mr,
           ss_lr, rs_lr, ss_t, rs_t):
    devices = rows * cols
    first, second, channels = x_ref.shape
    hidden = ow_ref.shape[1]
    fold = LANES // second
    depth = first // fold
    chunks = hidden // devices
    groups = cols // fold
    width = depth * LANES
    step = min(width, 512)
    my_row, my_col = lax.axis_index("row"), lax.axis_index("col")
    me = my_row * cols + my_col

    def partner(n):
        m = lax.rem(n * 13, devices) if devices % 13 else n
        return lax.rem(my_row + m % rows, rows), lax.rem(my_col + m // rows, cols)

    barrier = pltpu.get_barrier_semaphore()

    @pl.loop(1, devices)
    def _(n):
        pl.semaphore_signal(barrier, inc=1, device_id=partner(n), device_id_type=pl.DeviceIdType.MESH)

    for u in range(2):
        for p in range(4):
            turned = pw_ref[u, p].astype(f32).T.astype(bf16)
            for c in range(chunks):
                wt[u, c, p * devices:(p + 1) * devices, :] = turned[c * devices:(c + 1) * devices]
        gwt[u] = gw_ref[u].astype(f32).T.astype(bf16)
        owt[u] = ow_ref[u].astype(f32).T.astype(bf16)
    size = fold * LANES
    to = lax.broadcasted_iota(jnp.int32, (size, size), 1)
    at = lax.broadcasted_iota(jnp.int32, (size, size), 0)
    wanted = (to % LANES) // second * LANES + to // LANES * second + to % second
    perm[...] = jnp.where(at == wanted, 1.0, 0.0).astype(bf16)
    for q in range(depth):
        tile = jnp.concatenate([x_ref[a * depth + q] for a in range(fold)], axis=0)
        xt[:, q * LANES:(q + 1) * LANES] = tile.astype(f32).T

    def start(send, recv, ssem, rsem, slot):
        pltpu.make_async_copy(send.at[slot, me], recv.at[slot, me], rsem.at[slot]).start()

        @pl.loop(1, devices)
        def _(n):
            row, col = partner(n)
            pltpu.make_async_remote_copy(
                src_ref=send.at[slot, row * cols + col],
                dst_ref=recv.at[slot, me],
                send_sem=ssem.at[slot],
                recv_sem=rsem.at[slot],
                device_id=(row, col),
                device_id_type=pl.DeviceIdType.MESH,
            ).start()

    for u in range(2):
        gain_in = jnp.broadcast_to(ig_ref[u:u + 1, :], (LANES, channels)).T[:, :1]
        gain_out = jnp.broadcast_to(og_ref[u:u + 1, :], (LANES, hidden)).T[:, :1]
        for t in range(0, width, step):
            nt[:, t:t + step] = norm_columns(xt[:, t:t + step], gain_in).astype(bf16)
        for c in range(chunks):
            slot = u * chunks + c
            for t in range(0, width, step):
                got = jnp.dot(wt[u, c], nt[:, t:t + step], preferred_element_type=f32)
                for s in range(2):
                    base = 2 * s * devices
                    hand = jax.nn.sigmoid(got[base:base + devices]) * got[base + devices:base + 2 * devices]
                    for k in range(step // LANES):
                        shuffle[s, pl.ds(t // LANES + k, devices, stride=depth), :] = (
                            hand[:, k * LANES:(k + 1) * LANES]
                        )
            for s in range(2):
                send_lr[slot, :, s] = shuffle[s].reshape(devices, depth, LANES).astype(bf16)
            if slot == 0:
                pl.semaphore_wait(barrier, devices - 1)
            start(send_lr, recv_lr, ss_lr, rs_lr, slot)
        for t in range(0, width, step):
            gt[:, t:t + step] = jax.nn.sigmoid(
                jnp.dot(gwt[u], nt[:, t:t + step], preferred_element_type=f32)
            )
        for c in range(chunks):
            slot = u * chunks + c
            pltpu.make_async_copy(recv_lr.at[slot], recv_lr.at[slot], rs_lr.at[slot]).wait()
            for s, matrix in enumerate((ml, mr)):
                wide = jnp.concatenate([
                    jnp.concatenate([
                        recv_lr[slot, r * cols + g * fold + e, s]
                        for r in range(rows) for g in range(groups)
                    ], axis=0)
                    for e in range(fold)
                ], axis=1)
                moved = jnp.dot(wide, perm[...], preferred_element_type=f32).astype(bf16)
                for r in range(rows):
                    for g in range(groups):
                        for a in range(fold):
                            matrix[r * first + a * depth:r * first + (a + 1) * depth,
                                   g * LANES:(g + 1) * LANES] = (
                                moved[(r * groups + g) * depth:(r * groups + g + 1) * depth,
                                      a * LANES:(a + 1) * LANES]
                            )
            axis = 1 if u == 0 else 0
            tri = lax.dot_general(
                ml[...], mr[...], (((axis,), (axis,)), ((), ())), preferred_element_type=f32
            ).astype(bf16)
            wide = jnp.concatenate([
                jnp.concatenate([
                    tri[r * first + a * depth:r * first + (a + 1) * depth, g * LANES:(g + 1) * LANES]
                    for r in range(rows) for g in range(groups)
                ], axis=0)
                for a in range(fold)
            ], axis=1)
            moved = jnp.dot(wide, perm[...], preferred_element_type=f32).astype(bf16)
            for r in range(rows):
                for g in range(groups):
                    for e in range(fold):
                        send_t[slot, r * cols + g * fold + e] = (
                            moved[(r * groups + g) * depth:(r * groups + g + 1) * depth,
                                  e * LANES:(e + 1) * LANES]
                        )
            start(send_t, recv_t, ss_t, rs_t, slot)
        for c in range(chunks):
            slot = u * chunks + c
            pltpu.make_async_copy(recv_t.at[slot], recv_t.at[slot], rs_t.at[slot]).wait()
            back[...] = recv_t[slot].astype(f32).reshape(devices * depth, LANES)
            for q in range(depth):
                tt[c * devices:(c + 1) * devices, q * LANES:(q + 1) * LANES] = (
                    back[pl.ds(q, devices, stride=depth), :]
                )
        for t in range(0, width, step):
            mixed = norm_columns(tt[:, t:t + step], gain_out).astype(bf16)
            update = jnp.dot(owt[u], mixed, preferred_element_type=f32)
            xt[:, t:t + step] = (
                (xt[:, t:t + step] + gt[:, t:t + step] * update).astype(bf16).astype(f32)
            )
    for q in range(depth):
        tile = xt[:, q * LANES:(q + 1) * LANES].T.astype(bf16)
        for a in range(fold):
            o_ref[a * depth + q] = tile[a * second:(a + 1) * second]
    for slot in range(2 * chunks):
        for send, ssem in ((send_lr, ss_lr), (send_t, ss_t)):
            sent = send.at[slot, pl.ds(0, devices - 1)]
            pltpu.make_async_copy(sent, sent, ssem.at[slot]).wait()


def takes(rows, cols, first, second, channels, hidden):
    devices = rows * cols
    if LANES % second or second > LANES or channels != LANES or hidden % devices or devices % PACK:
        return False
    fold = LANES // second
    return (
        first % fold == 0 and (first // fold) % PACK == 0 and cols % fold == 0
        and hidden * first * second * 4 <= 2 ** 21
    )


def solution(mesh):
    rows, cols = mesh.shape["row"], mesh.shape["col"]

    def local(pair_rep, proj_weight, gate_weight, out_weight, in_gain, out_gain):
        first, second, channels = pair_rep.shape
        hidden = out_weight.shape[1]
        args = (pair_rep, proj_weight, gate_weight, out_weight, in_gain, out_gain)
        if not takes(rows, cols, first, second, channels, hidden):
            return plain(*args)
        devices = rows * cols
        fold = LANES // second
        depth = first // fold
        chunks = hidden // devices
        width = depth * LANES
        vmem = pl.BlockSpec(memory_space=pltpu.VMEM)
        return pl.pallas_call(
            functools.partial(kernel, rows, cols),
            out_shape=jax.ShapeDtypeStruct(pair_rep.shape, bf16),
            in_specs=[vmem] * 6,
            out_specs=vmem,
            scratch_shapes=[
                pltpu.VMEM((channels, width), f32),
                pltpu.VMEM((channels, width), bf16),
                pltpu.VMEM((channels, width), f32),
                pltpu.VMEM((hidden, width), f32),
                pltpu.VMEM((2, chunks, 4 * devices, channels), bf16),
                pltpu.VMEM((2, channels, channels), bf16),
                pltpu.VMEM((2, channels, hidden), bf16),
                pltpu.VMEM((fold * LANES, fold * LANES), bf16),
                pltpu.VMEM((2, devices * depth, LANES), f32),
                pltpu.VMEM((devices * depth, LANES), f32),
                pltpu.VMEM((2 * chunks, devices, 2, depth, LANES), bf16),
                pltpu.VMEM((2 * chunks, devices, 2, depth, LANES), bf16),
                pltpu.VMEM((2 * chunks, devices, depth, LANES), bf16),
                pltpu.VMEM((2 * chunks, devices, depth, LANES), bf16),
                pltpu.VMEM((rows * first, cols * second), bf16),
                pltpu.VMEM((rows * first, cols * second), bf16),
                pltpu.SemaphoreType.DMA((2 * chunks,)),
                pltpu.SemaphoreType.DMA((2 * chunks,)),
                pltpu.SemaphoreType.DMA((2 * chunks,)),
                pltpu.SemaphoreType.DMA((2 * chunks,)),
            ],
            compiler_params=pltpu.CompilerParams(collective_id=0, has_side_effects=True),
        )(*args)

    return jax.shard_map(
        local,
        mesh=mesh,
        in_specs=(P("row", "col", None), P(), P(), P(), P(), P()),
        out_specs=P("row", "col", None),
        check_vma=False,
    )
```

time: 205 us -> 85.2 us (0.42)
  blocking collectives: 91.3 us -> 0 us
  Pallas kernels: 0 us -> 83.1 us
  waiting for transfers between devices: 43.4 us -> 0 us
  local copies, waits for them, and re-layouts: 30.4 us -> 1.87 us
  between operations: 13.8 us -> 0.01 us
  matrix products: 10.6 us -> 0 us
  starting transfers between devices: 8.32 us -> 0 us
  other arithmetic: 6.98 us -> 0 us
    all_to_all x5 -> x0, blocking collectives: 91.3 us -> none  [the longest x2 39.2 us: local(): lax.all_to_all(right_hand, 'col', split_axis=0, concat_axis=2, tiled=True)]
    pallas_call x0 -> x1, Pallas kernels: none -> 83.1 us  [local(): pl.pallas_call(functools.partial(kernel, rows, cols), out_shape=jax.Shape...]
    all_to_all x2 -> x0, waiting for transfers between devices: 30 us -> none  [local(): lax.all_to_all(triangle.astype(jnp.bfloat16), 'col', split_axis=2, concat...]
    all_gather x2 -> x0, waiting for transfers between devices: 13.4 us -> none  [local(): lax.all_gather(right_rows, 'row', axis=1, tiled=True)]
    convert_element_type x10 -> x0, local copies, waits for them, and re-layouts: 12 us -> none  [the longest x2 3.39 us: local(): (jax.nn.sigmoid(projected[2]) * projected[3]).astype(jnp.bfloat16)]
    dot_general x8 -> x0, matrix products: 10.6 us -> none  [the longest x2 2.85 us: local(): jnp.dot(normed, gate_weight[update_index], preferred_element_type=jnp.flo...]
    unnamed x24 -> x1, local copies, waits for them, and re-layouts: 11.3 us -> 1.87 us
    all_to_all x2 -> x0, starting transfers between devices: 8.1 us -> none  [local(): lax.all_to_all(triangle.astype(jnp.bfloat16), 'col', split_axis=2, concat...]
  transfers between devices with their start and end apart: 4 -> 0, of which waited for: 3 -> 0; matrix products, arithmetic and copies ran while one was open for 5% -> 0% of each run, Pallas kernels for 0% -> 0%
where the time goes in v1:
time: 85.2 us; the launch traced here: 85 us
  Pallas kernels  83.1 us (98%)
  local copies, waits for them, and re-layouts  1.87 us (2%)
    pallas_call x1, Pallas kernels, local(): pl.pallas_call(functools.partial(kernel, rows, cols), out_shape=jax.Shape...  83.1 us
    unnamed x1, local copies, waits for them, and re-layouts  1.87 us

profile of v1, /device:TPU:0, one launch (start us, length us, event | category | flops | bytes accessed | tf_op | source)
XLA Modules:
  0.0 85.0 jit_solution(15902953226858657677)
XLA Ops:
  0.0 83.1 %shard_map.64 = bf16[64,32,128]{2,1,0:T(8,128)(2,1)} custom-call(bf16[64,32,128]{2,1,0:T(8,128)(2,1)} %x_ref.1, bf16[2,4,128,128]{3,2,1,0:T(8,128)(2,1)} %pw_ref.1, bf16[2,128,128]{2,1,0:T(8,128)(2,1)} %gw_ref.1, bf16[2,128,128]{2,1,0:T(8,128)(2,1)} %ow_ref.1, f32[2,128]{1,0:T(2,128)} %ig_ref.1, f32[2,128]{1,0:T(2,128)} %og_ref.1), custom_call_target="tpu_custom_call" | custom-call | tf_op jit(solution)/shard_map/pallas_call | solution.py:247
  83.1 1.9 %copy.8 = bf16[64,32,128]{2,1,0:T(8,128)(2,1)} copy(bf16[64,32,128]{2,1,0:T(8,128)(2,1)} %shard_map.64) | data formatting | bytes 1048576

commit v2 on v1

v2 whole, which is shorter than its diff:
```python
import functools

import jax
import jax.numpy as jnp
from jax import lax
from jax.experimental import pallas as pl
from jax.experimental.pallas import tpu as pltpu
from jax.sharding import PartitionSpec as P

epsilon = 1e-05
LANES = 128
PACK = 16
CHUNK = 32
f32 = jnp.float32
bf16 = jnp.bfloat16


def layer_norm(values, gain_row, reduce_axis):
    center = values - jnp.mean(values, axis=reduce_axis, keepdims=True)
    spread = jnp.mean(center * center, axis=reduce_axis, keepdims=True)
    return center * lax.rsqrt(spread + epsilon) * gain_row


def plain(pair_rep, proj_weight, gate_weight, out_weight, in_gain, out_gain):
    current = pair_rep
    for update_index in range(2):
        widened = current.astype(f32)
        normed = layer_norm(widened, in_gain[update_index], 2).astype(bf16)
        projected = jnp.einsum(
            "ijc,pch->phij", normed, proj_weight[update_index], preferred_element_type=f32
        )
        left_hand = (jax.nn.sigmoid(projected[0]) * projected[1]).astype(bf16)
        right_hand = (jax.nn.sigmoid(projected[2]) * projected[3]).astype(bf16)
        gating = jax.nn.sigmoid(
            jnp.dot(normed, gate_weight[update_index], preferred_element_type=f32)
        )
        left_rows, right_rows = (
            lax.all_to_all(left_hand, "col", split_axis=0, concat_axis=2, tiled=True),
            lax.all_to_all(right_hand, "col", split_axis=0, concat_axis=2, tiled=True),
        )
        if update_index == 0:
            triangle = jnp.einsum(
                "gik,gjk->igj",
                left_rows,
                lax.all_gather(right_rows, "row", axis=1, tiled=True),
                preferred_element_type=f32,
            )
        else:
            left_columns = lax.all_to_all(left_rows, "row", split_axis=2, concat_axis=1, tiled=True)
            triangle = jnp.einsum(
                "gki,gkj->igj",
                left_columns,
                lax.all_gather(right_rows, "row", axis=1, tiled=True),
                preferred_element_type=f32,
            )
        returned = lax.all_to_all(
            triangle.astype(bf16), "col", split_axis=2, concat_axis=1, tiled=True
        )
        mixed_rows = layer_norm(
            returned.astype(f32), out_gain[update_index][None, :, None], 1
        ).astype(bf16)
        update = jnp.einsum(
            "ihj,hc->ijc", mixed_rows, out_weight[update_index], preferred_element_type=f32
        )
        current = (widened + gating * update).astype(bf16)
    return current


def norm_columns(values, gain_column):
    scale = 1.0 / values.shape[0]
    center = values - jnp.sum(values, axis=0, keepdims=True) * scale
    spread = jnp.sum(center * center, axis=0, keepdims=True) * scale
    return center * lax.rsqrt(spread + epsilon) * gain_column


def kernel(rows, cols, x_ref, pw_ref, gw_ref, ow_ref, ig_ref, og_ref, o_ref,
           xt, nt, gt, tt, wt, gwt, owt, perm, shuffle, back,
           send_h, recv_h0, recv_l1, recv_r1, send_t0, recv_t0, send_t1, recv_t1, ml, mr, sems):
    first, second, channels = x_ref.shape
    hidden = ow_ref.shape[1]
    side = cols // 2
    team = rows * side
    fold = LANES // second
    depth = first // fold
    block = CHUNK
    chunks = hidden // block
    each = block // team
    groups = side // fold
    width = depth * LANES
    step = min(width, 512)
    my_row, my_col = lax.axis_index("row"), lax.axis_index("col")
    my_half, my_side = my_col // side, my_col % side
    me = my_row * side + my_side

    def mate(n):
        m = (n * 13) % team if team % 13 else n
        row, place = (my_row + m % rows) % rows, (my_side + m // rows) % side
        return row, place

    def device(n, other):
        row, place = mate(n)
        return row, (1 - my_half if other else my_half) * side + place

    barrier = pltpu.get_barrier_semaphore()

    def greet(n, other):
        pl.semaphore_signal(
            barrier, inc=1, device_id=device(n, other), device_id_type=pl.DeviceIdType.MESH
        )

    greet(0, True)

    @pl.loop(1, team)
    def _(n):
        greet(n, True)
        greet(n, False)

    def send(source, target, kind, slot, n, other):
        row, place = mate(n)
        pltpu.make_async_remote_copy(
            src_ref=source(row, place, other),
            dst_ref=target,
            send_sem=sems.at[2 * kind, slot],
            recv_sem=sems.at[2 * kind + 1, slot],
            device_id=device(n, other),
            device_id_type=pl.DeviceIdType.MESH,
        ).start()

    def keep(source, target, kind, slot):
        pltpu.make_async_copy(
            source(my_row, my_side, False), target, sems.at[2 * kind + 1, slot]
        ).start()

    def arrive(buffer, kind, slot):
        pltpu.make_async_copy(buffer, buffer, sems.at[2 * kind + 1, slot]).wait()

    def weight_turn(u):
        for p in range(4):
            turned = pw_ref[u, p].astype(f32).T.astype(bf16)
            for c in range(chunks):
                wt[u, c, p * block:(p + 1) * block, :] = turned[c * block:(c + 1) * block]

    weight_turn(0)
    for q in range(depth):
        tile = jnp.concatenate([x_ref[a * depth + q] for a in range(fold)], axis=0)
        xt[:, q * LANES:(q + 1) * LANES] = tile.astype(f32).T

    def rest_of_setup():
        weight_turn(1)
        for u in range(2):
            gwt[u] = gw_ref[u].astype(f32).T.astype(bf16)
            owt[u] = ow_ref[u].astype(f32).T.astype(bf16)
        size = fold * LANES
        bits, low = LANES.bit_length() - 1, second.bit_length() - 1
        to = lax.broadcasted_iota(jnp.int32, (1, size), 1)
        at = lax.broadcasted_iota(jnp.int32, (size, size), 0)
        wanted = (
            (((to & (LANES - 1)) >> low) << bits) + ((to >> bits) << low) + (to & (second - 1))
        )
        perm[...] = jnp.where(at == wanted, 1.0, 0.0).astype(bf16)

    def regroup(parts):
        wide = jnp.concatenate([jnp.concatenate(tiles, axis=0) for tiles in parts], axis=1)
        return jnp.dot(wide, perm[...], preferred_element_type=f32).astype(bf16)

    def tile_of(array, row, lane):
        return array[row * depth:(row + 1) * depth, lane * LANES:(lane + 1) * LANES]

    for u in range(2):
        gain_in = jnp.broadcast_to(ig_ref[u:u + 1, :], (LANES, channels)).T[:, :1]
        gain_out = jnp.broadcast_to(og_ref[u:u + 1, :], (LANES, hidden)).T[:, :1]
        for t in range(0, width, step):
            nt[:, t:t + step] = norm_columns(xt[:, t:t + step], gain_in).astype(bf16)
        for c in range(chunks):
            for t in range(0, width, step):
                got = jnp.dot(wt[u, c], nt[:, t:t + step], preferred_element_type=f32)
                for s in range(2):
                    base = 2 * s * block
                    hand = jax.nn.sigmoid(got[base:base + block]) * got[base + block:base + 2 * block]
                    for k in range(step // LANES):
                        shuffle[s, pl.ds(t // LANES + k, block, stride=depth), :] = (
                            hand[:, k * LANES:(k + 1) * LANES]
                        )
            for s in range(2):
                send_h[u, c, :, s] = shuffle[s].reshape(team, each, depth, LANES).astype(bf16)
            if u == 0:
                if c == 0:
                    pl.semaphore_wait(barrier, 2 * team - 1)
                both = lambda row, place, other: send_h.at[0, c, row * side + place]
                keep(both, recv_h0.at[c, me], 0, c)

                @pl.loop(1, team)
                def _(n):
                    send(both, recv_h0.at[c, me], 0, c, n, False)
            else:
                left = lambda row, place, other: send_h.at[1, c, row * side + place, 0]
                right = lambda row, place, other: send_h.at[1, c, row * side + place, 1]
                keep(left, recv_l1.at[c, my_half * team + me], 1, c)
                keep(right, recv_r1.at[c, me], 2, c)
                send(left, recv_l1.at[c, my_half * team + me], 1, c, 0, True)

                @pl.loop(1, team)
                def _(n):
                    send(left, recv_l1.at[c, my_half * team + me], 1, c, n, True)
                    send(left, recv_l1.at[c, my_half * team + me], 1, c, n, False)
                    send(right, recv_r1.at[c, me], 2, c, n, False)
        if u == 0:
            rest_of_setup()
        for t in range(0, width, step):
            gt[:, t:t + step] = jax.nn.sigmoid(
                jnp.dot(gwt[u], nt[:, t:t + step], preferred_element_type=f32)
            )
        for c in range(chunks):
            if u == 0:
                arrive(recv_h0.at[c], 0, c)
                sources = [
                    (matrix, e, 0, lambda d, s=s, e=e: recv_h0[c, d, s, e])
                    for s, matrix in enumerate((ml, mr)) for e in range(each)
                ]
            else:
                arrive(recv_l1.at[c], 1, c)
                arrive(recv_r1.at[c], 2, c)
                sources = [
                    (ml, e, h, lambda d, h=h, e=e: recv_l1[c, h * team + d, e])
                    for h in range(2) for e in range(each)
                ] + [(mr, e, 0, lambda d, e=e: recv_r1[c, d, e]) for e in range(each)]
            moved = regroup([
                [
                    get(r * side + g * fold + i)
                    for _, _, _, get in sources for r in range(rows) for g in range(groups)
                ]
                for i in range(fold)
            ])
            at = 0
            for matrix, e, h, _ in sources:
                for r in range(rows):
                    for g in range(groups):
                        lane = (h * groups + g) * LANES
                        for a in range(fold):
                            matrix[e, r * first + a * depth:r * first + (a + 1) * depth,
                                   lane:lane + LANES] = tile_of(moved, at, a)
                        at += 1
            wide_groups = 2 * groups if u == 0 else groups
            triangles = []
            for e in range(each):
                if u == 0:
                    pair = ml[e, :, :groups * LANES], mr[e]
                    over = (((1,), (1,)), ((), ()))
                else:
                    pair = ml[e], mr[e]
                    over = (((0,), (0,)), ((), ()))
                triangles.append(
                    lax.dot_general(*pair, over, preferred_element_type=f32).astype(bf16)
                )
            moved = regroup([
                [
                    tile_of(triangles[e], r * fold + a, g)
                    for e in range(each) for r in range(rows) for g in range(wide_groups)
                ]
                for a in range(fold)
            ])
            at = 0
            out = send_t0 if u == 0 else send_t1
            for e in range(each):
                for r in range(rows):
                    for g in range(wide_groups):
                        for i in range(fold):
                            place = g * fold + i
                            half, place = place // side, place % side
                            tile = tile_of(moved, at, i)
                            if u == 0:
                                out[c, half, r * side + place, e] = tile
                            else:
                                out[c, r * side + place, e] = tile
                        at += 1
            if u == 0:
                sums = lambda row, place, other: send_t0.at[
                    c, 1 - my_half if other else my_half, row * side + place
                ]
                keep(sums, recv_t0.at[c, my_half * team + me], 3, c)
                send(sums, recv_t0.at[c, my_half * team + me], 3, c, 0, True)

                @pl.loop(1, team)
                def _(n):
                    send(sums, recv_t0.at[c, my_half * team + me], 3, c, n, True)
                    send(sums, recv_t0.at[c, my_half * team + me], 3, c, n, False)
            else:
                made = lambda row, place, other: send_t1.at[c, row * side + place]
                keep(made, recv_t1.at[c, me], 4, c)

                @pl.loop(1, team)
                def _(n):
                    send(made, recv_t1.at[c, me], 4, c, n, False)
        for c in range(chunks):
            if u == 0:
                arrive(recv_t0.at[c], 3, c)
                total = recv_t0[c, :team].astype(f32) + recv_t0[c, team:].astype(f32)
            else:
                arrive(recv_t1.at[c], 4, c)
                total = recv_t1[c].astype(f32)
            back[...] = total.reshape(block * depth, LANES)
            for q in range(depth):
                tt[c * block:(c + 1) * block, q * LANES:(q + 1) * LANES] = (
                    back[pl.ds(q, block, stride=depth), :]
                )
        for t in range(0, width, step):
            mixed = norm_columns(tt[:, t:t + step], gain_out).astype(bf16)
            update = jnp.dot(owt[u], mixed, preferred_element_type=f32)
            xt[:, t:t + step] = (
                (xt[:, t:t + step] + gt[:, t:t + step] * update).astype(bf16).astype(f32)
            )
    for q in range(depth):
        tile = xt[:, q * LANES:(q + 1) * LANES].T.astype(bf16)
        for a in range(fold):
            o_ref[a * depth + q] = tile[a * second:(a + 1) * second]

    def gone(buffer, kind, slot):
        pltpu.make_async_copy(buffer, buffer, sems.at[2 * kind, slot]).wait()

    for c in range(chunks):
        gone(recv_h0.at[c, pl.ds(0, team - 1)], 0, c)
        gone(recv_l1.at[c, pl.ds(0, 2 * team - 1)], 1, c)
        gone(recv_r1.at[c, pl.ds(0, team - 1)], 2, c)
        gone(recv_t0.at[c, pl.ds(0, 2 * team - 1)], 3, c)
        gone(recv_t1.at[c, pl.ds(0, team - 1)], 4, c)


def takes(rows, cols, first, second, channels, hidden):
    if LANES % second or channels != LANES or hidden != LANES or cols % 2:
        return False
    team, fold = rows * (cols // 2), LANES // second
    return (
        CHUNK % team == 0 and first % fold == 0 and (first // fold) % PACK == 0
        and (cols // 2) % fold == 0 and first * second <= 2048
    )


def solution(mesh):
    rows, cols = mesh.shape["row"], mesh.shape["col"]

    def local(pair_rep, proj_weight, gate_weight, out_weight, in_gain, out_gain):
        first, second, channels = pair_rep.shape
        hidden = out_weight.shape[1]
        args = (pair_rep, proj_weight, gate_weight, out_weight, in_gain, out_gain)
        if not takes(rows, cols, first, second, channels, hidden):
            return plain(*args)
        team = rows * (cols // 2)
        fold = LANES // second
        depth = first // fold
        chunks = hidden // CHUNK
        each = CHUNK // team
        width = depth * LANES
        vmem = pl.BlockSpec(memory_space=pltpu.VMEM)
        return pl.pallas_call(
            functools.partial(kernel, rows, cols),
            out_shape=jax.ShapeDtypeStruct(pair_rep.shape, bf16),
            in_specs=[vmem] * 6,
            out_specs=vmem,
            scratch_shapes=[
                pltpu.VMEM((channels, width), f32),
                pltpu.VMEM((channels, width), bf16),
                pltpu.VMEM((channels, width), f32),
                pltpu.VMEM((hidden, width), f32),
                pltpu.VMEM((2, chunks, 4 * CHUNK, channels), bf16),
                pltpu.VMEM((2, channels, channels), bf16),
                pltpu.VMEM((2, channels, hidden), bf16),
                pltpu.VMEM((fold * LANES, fold * LANES), bf16),
                pltpu.VMEM((2, CHUNK * depth, LANES), f32),
                pltpu.VMEM((CHUNK * depth, LANES), f32),
                pltpu.VMEM((2, chunks, team, 2, each, depth, LANES), bf16),
                pltpu.VMEM((chunks, team, 2, each, depth, LANES), bf16),
                pltpu.VMEM((chunks, 2 * team, each, depth, LANES), bf16),
                pltpu.VMEM((chunks, team, each, depth, LANES), bf16),
                pltpu.VMEM((chunks, 2, team, each, depth, LANES), bf16),
                pltpu.VMEM((chunks, 2 * team, each, depth, LANES), bf16),
                pltpu.VMEM((chunks, team, each, depth, LANES), bf16),
                pltpu.VMEM((chunks, team, each, depth, LANES), bf16),
                pltpu.VMEM((each, rows * first, cols * second), bf16),
                pltpu.VMEM((each, rows * first, cols // 2 * second), bf16),
                pltpu.SemaphoreType.DMA((10, chunks)),
            ],
            compiler_params=pltpu.CompilerParams(collective_id=0, has_side_effects=True),
        )(*args)

    return jax.shard_map(
        local,
        mesh=mesh,
        in_specs=(P("row", "col", None), P(), P(), P(), P(), P()),
        out_specs=P("row", "col", None),
        check_vma=False,
    )
```

time: 85.2 us -> 76.1 us (0.89)
  Pallas kernels: 83.1 us -> 74.1 us
    pallas_call x1, Pallas kernels: 83.1 us -> 74.1 us  [local(): pl.pallas_call(functools.partial(kernel, rows, cols), out_shape=jax.Shape...]
where the time goes in v2:
time: 76.1 us; the launch traced here: 76 us
  Pallas kernels  74.1 us (97%)
  local copies, waits for them, and re-layouts  1.87 us (2%)
    pallas_call x1, Pallas kernels, local(): pl.pallas_call(functools.partial(kernel, rows, cols), out_shape=jax.Shape...  74.1 us
    unnamed x1, local copies, waits for them, and re-layouts  1.87 us

profile of v2, /device:TPU:0, one launch (start us, length us, event | category | flops | bytes accessed | tf_op | source)
XLA Modules:
  0.0 76.0 jit_solution(18002887860879327086)
XLA Ops:
  0.0 74.1 %shard_map.64 = bf16[64,32,128]{2,1,0:T(8,128)(2,1)} custom-call(bf16[64,32,128]{2,1,0:T(8,128)(2,1)} %x_ref.1, bf16[2,4,128,128]{3,2,1,0:T(8,128)(2,1)} %pw_ref.1, bf16[2,128,128]{2,1,0:T(8,128)(2,1)} %gw_ref.1, bf16[2,128,128]{2,1,0:T(8,128)(2,1)} %ow_ref.1, f32[2,128]{1,0:T(2,128)} %ig_ref.1, f32[2,128]{1,0:T(2,128)} %og_ref.1), custom_call_target="tpu_custom_call" | custom-call | tf_op jit(solution)/shard_map/pallas_call | solution.py:354
  74.1 1.9 %copy.8 = bf16[64,32,128]{2,1,0:T(8,128)(2,1)} copy(bf16[64,32,128]{2,1,0:T(8,128)(2,1)} %shard_map.64) | data formatting | bytes 1048576

commit v3 on v2

--- a/solution.py
+++ b/solution.py
@@ -10,7 +10,7 @@
 epsilon = 1e-05
 LANES = 128
 PACK = 16
-CHUNK = 32
+CHUNK = 16
 f32 = jnp.float32
 bf16 = jnp.bfloat16
 
@@ -309,10 +309,7 @@
             xt[:, t:t + step] = (
                 (xt[:, t:t + step] + gt[:, t:t + step] * update).astype(bf16).astype(f32)
             )
-    for q in range(depth):
-        tile = xt[:, q * LANES:(q + 1) * LANES].T.astype(bf16)
-        for a in range(fold):
-            o_ref[a * depth + q] = tile[a * second:(a + 1) * second]
+    o_ref[...] = xt[...].astype(bf16)
 
     def gone(buffer, kind, slot):
         pltpu.make_async_copy(buffer, buffer, sems.at[2 * kind, slot]).wait()
@@ -323,6 +320,15 @@
         gone(recv_r1.at[c, pl.ds(0, team - 1)], 2, c)
         gone(recv_t0.at[c, pl.ds(0, 2 * team - 1)], 3, c)
         gone(recv_t1.at[c, pl.ds(0, team - 1)], 4, c)
+
+
+def finish(fold, t_ref, o_ref):
+    first, second, _ = o_ref.shape
+    depth = first // fold
+    for q in range(depth):
+        tile = t_ref[:, q * LANES:(q + 1) * LANES].astype(f32).T.astype(bf16)
+        for a in range(fold):
+            o_ref[a * depth + q] = tile[a * second:(a + 1) * second]
 
 
 def takes(rows, cols, first, second, channels, hidden):
@@ -351,9 +357,9 @@
         each = CHUNK // team
         width = depth * LANES
         vmem = pl.BlockSpec(memory_space=pltpu.VMEM)
-        return pl.pallas_call(
+        turned = pl.pallas_call(
             functools.partial(kernel, rows, cols),
-            out_shape=jax.ShapeDtypeStruct(pair_rep.shape, bf16),
+            out_shape=jax.ShapeDtypeStruct((channels, width), bf16),
             in_specs=[vmem] * 6,
             out_specs=vmem,
             scratch_shapes=[
@@ -381,6 +387,12 @@
             ],
             compiler_params=pltpu.CompilerParams(collective_id=0, has_side_effects=True),
         )(*args)
+        return pl.pallas_call(
+            functools.partial(finish, fold),
+            out_shape=jax.ShapeDtypeStruct(pair_rep.shape, bf16),
+            in_specs=[vmem],
+            out_specs=vmem,
+        )(turned)
 
     return jax.shard_map(
         local,

time: 76.1 us -> 75.4 us (level)
  local copies, waits for them, and re-layouts: 1.87 us -> 0 us
  Pallas kernels: 74.1 us -> 75.2 us
    pallas_call x0 -> x1, Pallas kernels: none -> 2.04 us  [local(): pl.pallas_call(functools.partial(finish, fold), out_shape=jax.ShapeDtypeS...]
    unnamed x1 -> x0, local copies, waits for them, and re-layouts: 1.87 us -> none
    pallas_call x1, Pallas kernels: 74.1 us -> 73.2 us  [local(): pl.pallas_call(functools.partial(kernel, rows, cols), out_shape=jax.Shape...]
where the time goes in v3:
time: 75.4 us; the launch traced here: 75.2 us
  Pallas kernels  75.2 us (100%)
    pallas_call x1, Pallas kernels, local(): pl.pallas_call(functools.partial(kernel, rows, cols), out_shape=jax.Shape...  73.2 us
    pallas_call x1, Pallas kernels, local(): pl.pallas_call(functools.partial(finish, fold), out_shape=jax.ShapeDtypeS...  2.04 us

profile of v3, /device:TPU:0, one launch (start us, length us, event | category | flops | bytes accessed | tf_op | source)
XLA Modules:
  0.0 75.2 jit_solution(12641667943974705715)
XLA Ops:
  0.0 73.2 %shard_map.64.t_ref = bf16[128,2048]{1,0:T(8,128)(2,1)} custom-call(bf16[64,32,128]{2,1,0:T(8,128)(2,1)} %x_ref.1, bf16[2,4,128,128]{3,2,1,0:T(8,128)(2,1)} %pw_ref.1, bf16[2,128,128]{2,1,0:T(8,128)(2,1)} %gw_ref.1, bf16[2,128,128]{2,1,0:T(8,128)(2,1)} %ow_ref.1, f32[2,128]{1,0:T(2,128)} %ig_ref.1, f32[2,128]{1,0:T(2,128)} %og_ref.1), custom_call_target="tpu_custom_call" | custom-call | tf_op jit(solution)/shard_map/pallas_call | solution.py:360
  73.2 2.0 %shard_map.65 = bf16[64,32,128]{2,1,0:T(8,128)(2,1)} custom-call(bf16[128,2048]{1,0:T(8,128)(2,1)} %shard_map.64.t_ref), custom_call_target="tpu_custom_call" | custom-call | tf_op jit(solution)/shard_map/pallas_call | solution.py:390
